TPU v7x, 32 devices: a whole 2x2x4 slice. The times are simulated.
32 devices in a mesh: dp: 8 (over y, x, core), mp: 4 (over z).
Axes of the slice: x: 2, y: 2, z: 4, core: 2. Of those that a mesh axis runs over, the one named last changes fastest.
Arguments:
- tokens: bfloat16 [8192, 2048], P('dp'), may hold values from -6 to 6
- doc_lengths: int32 [8, 8], P('dp'), may hold values from 1 to 512, 1024 in all within a row
- slot_live: int32 [36], P('mp'), may hold values from 0 to 1, as said below
- attn_gain: bfloat16 [2048], replicated, may hold values from 0.5 to 1.5
- w_query: bfloat16 [2048, 1536], P(None, 'mp'), may hold values from -0.125 to 0.125
- w_keyval: bfloat16 [2048, 768], replicated, may hold values from -0.125 to 0.125
- q_gain: bfloat16 [64], replicated, may hold values from 0.099609375 to 1.8984375
- k_gain: bfloat16 [64], replicated, may hold values from 0.099609375 to 1.8984375
- w_out: bfloat16 [1536, 2048], P('mp'), may hold values from -0.625 to 0.625
- ffn_gain: bfloat16 [2048], replicated, may hold values from 0.5 to 1.5
- w_gate: bfloat16 [2048, 4608], P(None, 'mp'), may hold values from -0.125 to 0.125
- w_up: bfloat16 [2048, 4608], P(None, 'mp'), may hold values from -0.125 to 0.125
- w_down: bfloat16 [4608, 2048], P('mp'), may hold values from -0.09375 to 0.09375
- out_grad: bfloat16 [8192, 2048], P('dp'), may hold values from -6 to 6
Outputs:
- block_out: bfloat16 [8192, 2048], P(('dp', 'mp'))
- grad_tokens: float32 [8192, 2048], P(('dp', 'mp'))
- grad_attn_gain: float32 [2048], replicated
- grad_query: float32 [2048, 1536], P('dp', 'mp')
- grad_keyval: float32 [2048, 768], P(('dp', 'mp'))
- grad_q_gain: float32 [64], replicated
- grad_k_gain: float32 [64], replicated
- grad_out_proj: float32 [1536, 2048], P('mp', 'dp')
- grad_ffn_gain: float32 [2048], replicated
- grad_gate: float32 [2048, 4608], P('dp', 'mp')
- grad_up: float32 [2048, 4608], P('dp', 'mp')
- grad_down: float32 [4608, 2048], P('mp', 'dp')
Inputs may be any that keep to these rules, and one draw needn't show every extreme that they name: `doc_lengths`: each row's 8 lengths sum to 1024, and one of them is 512. `slot_live`: the 9 slots of each index of mp hold 34 // 4 or 34 // 4 + 1 live ones, 34 live in all; which slots and which indices hold more varies.
All inputs are finite; a program needn't handle non-finite values.
Results may differ from a plain program's by a relative error of at most 0.018.
Values may be sent and summed in bfloat16 or wider, within the bound.
A program may use at most 192 MiB of HBM per device.

v0:
```python
import math
import jax
import jax.numpy as jnp
from jax import lax
from jax.sharding import PartitionSpec as P

EPSILON = 1e-06
MASKED = -1000000000.0
ROPE_BASE = 10000.0
HIGHEST_PREC = lax.Precision.HIGHEST
CONTRACT_LAST = (((1,), (1,)), ((), ()))
CONTRACT_FIRST = (((0,), (0,)), ((), ()))


def normalize(raw_in):
    return raw_in * lax.rsqrt(jnp.mean(raw_in * raw_in, axis=-1, keepdims=True) + EPSILON)


def norm_back(grad_normed, raw_in, gain_vec):
    factor = lax.rsqrt(jnp.mean(raw_in * raw_in, axis=-1, keepdims=True) + EPSILON)
    unit_rows = raw_in * factor
    scaled = grad_normed * gain_vec
    grad_raw = factor * (scaled - unit_rows * jnp.mean(scaled * unit_rows, axis=-1, keepdims=True))
    return (grad_raw, jnp.sum(grad_normed * unit_rows, axis=tuple(range(raw_in.ndim - 1))))


def rotate(values, cosine_tab, sine_tab, sign):
    half_size = values.shape[-1] // 2
    first_half = values[..., :half_size]
    second_half = values[..., half_size:]
    return jnp.concatenate(
        [
            first_half * cosine_tab - sign * second_half * sine_tab,
            second_half * cosine_tab + sign * first_half * sine_tab,
        ],
        axis=-1,
    )


def doc_layout(lengths, row_count):
    doc_ends = jnp.cumsum(lengths)
    token_index = jnp.arange(row_count, dtype=jnp.int32)
    past_end = (token_index[:, None] >= doc_ends[None, :]).astype(jnp.int32)
    doc_id = jnp.sum(past_end, axis=1)
    doc_pos = token_index - jnp.sum(past_end * lengths[None, :], axis=1)
    return (doc_id, doc_pos, token_index)


def rope_table(doc_pos, head_size):
    rope_freq = jnp.exp(
        jnp.arange(head_size // 2, dtype=jnp.float32) * (-2.0 * math.log(ROPE_BASE) / head_size)
    )
    rope_angle = doc_pos.astype(jnp.float32)[:, None] * rope_freq[None, :]
    return (jnp.cos(rope_angle)[:, None, :], jnp.sin(rope_angle)[:, None, :])


def shards(
    tokens,
    doc_lengths,
    slot_live,
    attn_gain,
    w_query,
    w_keyval,
    q_gain,
    k_gain,
    w_out,
    ffn_gain,
    w_gate,
    w_up,
    w_down,
    out_grad,
):
    row_count, model_width = tokens.shape
    head_size = q_gain.shape[0]
    heads_dev = w_query.shape[1] // head_size
    heads_all = heads_dev * lax.axis_size("mp")
    kv_heads = w_keyval.shape[1] // (2 * head_size)
    group_size = heads_all // kv_heads
    kv_window = min(kv_heads, (heads_dev + group_size - 2) // group_size + 1)
    tile_cols = w_gate.shape[1] // slot_live.shape[0]
    shard_rows = row_count // lax.axis_size("mp")
    block_rows = min(512, row_count)
    score_scale = head_size ** (-0.5)
    head_span = heads_dev * head_size
    mp_index = lax.axis_index("mp")
    row_first = mp_index * shard_rows
    q_first = mp_index * heads_dev
    kv_first = jnp.minimum(q_first // group_size, kv_heads - kv_window)
    kv_owner = (q_first + jnp.arange(heads_dev, dtype=jnp.int32)) // group_size - kv_first
    head_pick = (kv_owner[:, None] == jnp.arange(kv_window, dtype=jnp.int32)[None, :]).astype(
        jnp.float32
    )
    key_cols = lax.dynamic_slice_in_dim(w_keyval, kv_first * head_size, kv_window * head_size, 1)
    value_cols = lax.dynamic_slice_in_dim(
        w_keyval, (kv_heads + kv_first) * head_size, kv_window * head_size, 1
    )

    def spread(window_cols):
        return (
            jnp.einsum(
                "dwe,hw->dhe",
                window_cols.reshape(model_width, kv_window, head_size),
                head_pick.astype(jnp.bfloat16),
                preferred_element_type=jnp.float32,
            )
            .astype(jnp.bfloat16)
            .reshape(model_width, head_span)
        )

    def fold_heads(per_head):
        return jnp.einsum(
            "dhe,hw->dwe",
            per_head.reshape(model_width, heads_dev, head_size),
            head_pick,
            precision=HIGHEST_PREC,
        ).reshape(model_width, kv_window * head_size)

    doc_id, doc_pos, token_index = doc_layout(doc_lengths[0], row_count)
    cosine_tab, sine_tab = rope_table(doc_pos, head_size)
    x_float = tokens.astype(jnp.float32)
    x_rows = lax.dynamic_slice_in_dim(x_float, row_first, shard_rows, 0)
    gain_one = attn_gain.astype(jnp.float32)
    gain_two = ffn_gain.astype(jnp.float32)
    q_gain_f = q_gain.astype(jnp.float32)
    k_gain_f = k_gain.astype(jnp.float32)
    xn_one = (normalize(x_float) * gain_one).astype(jnp.bfloat16)
    q_raw = jnp.dot(xn_one, w_query, preferred_element_type=jnp.float32).reshape(
        row_count, heads_dev, head_size
    )
    kv_raw = jnp.dot(
        xn_one, jnp.concatenate([key_cols, value_cols], axis=1), preferred_element_type=jnp.float32
    ).reshape(row_count, 2, kv_window, head_size)
    k_raw = jnp.einsum("twe,hw->the", kv_raw[:, 0], head_pick, precision=HIGHEST_PREC)
    v_raw = jnp.einsum("twe,hw->the", kv_raw[:, 1], head_pick, precision=HIGHEST_PREC)
    q_rot = rotate(normalize(q_raw) * q_gain_f, cosine_tab, sine_tab, 1.0).astype(jnp.bfloat16)
    k_rot = rotate(normalize(k_raw) * k_gain_f, cosine_tab, sine_tab, 1.0).astype(jnp.bfloat16)
    v_low = v_raw.astype(jnp.bfloat16)

    def block_scores(row_start, key_stop):
        scores = (
            jnp.einsum(
                "qhe,khe->hqk",
                q_rot[row_start : row_start + block_rows],
                k_rot[:key_stop],
                preferred_element_type=jnp.float32,
            )
            * score_scale
        )
        allowed = (doc_id[row_start : row_start + block_rows, None] == doc_id[None, :key_stop]) & (
            token_index[None, :key_stop] <= token_index[row_start : row_start + block_rows, None]
        )
        return jnp.where(allowed[None], scores, MASKED)

    block_outs = []
    block_lse = []
    for row_start in range(0, row_count, block_rows):
        key_stop = row_start + block_rows
        scores = block_scores(row_start, key_stop)
        row_max = jnp.max(scores, axis=-1, keepdims=True)
        shifted = jnp.exp(scores - row_max)
        row_total = jnp.sum(shifted, axis=-1, keepdims=True)
        attn_probs = (shifted / row_total).astype(jnp.bfloat16)
        block_outs.append(
            jnp.einsum(
                "hqk,khe->qhe", attn_probs, v_low[:key_stop], preferred_element_type=jnp.float32
            )
        )
        block_lse.append(row_max + jnp.log(row_total))
    attended = (
        jnp.concatenate(block_outs, axis=0).reshape(row_count, head_span).astype(jnp.bfloat16)
    )
    attn_part = jnp.dot(attended, w_out, preferred_element_type=jnp.float32)
    hidden_full = x_float + lax.psum(attn_part, "mp")
    hidden_rows = lax.dynamic_slice_in_dim(hidden_full, row_first, shard_rows, 0)
    xn_two = (normalize(hidden_full) * gain_two).astype(jnp.bfloat16)
    live_cols = jnp.repeat(slot_live.astype(jnp.float32), tile_cols)
    gate_act = jnp.dot(xn_two, w_gate, preferred_element_type=jnp.float32)
    up_act = jnp.dot(xn_two, w_up, preferred_element_type=jnp.float32)
    gate_sigmoid = jax.nn.sigmoid(gate_act)
    gate_silu = gate_act * gate_sigmoid
    ffn_hidden = (gate_silu * up_act * live_cols).astype(jnp.bfloat16)
    ffn_part = jnp.dot(ffn_hidden, w_down, preferred_element_type=jnp.float32)
    out_rows = hidden_rows + lax.psum_scatter(
        ffn_part.astype(jnp.bfloat16), "mp", scatter_dimension=0, tiled=True
    ).astype(jnp.float32)
    block_out = out_rows.astype(jnp.bfloat16)
    d_hidden = (
        lax.dot_general(out_grad, w_down, CONTRACT_LAST, preferred_element_type=jnp.float32)
        * live_cols
    )
    grad_down = lax.dot_general(
        ffn_hidden, out_grad, CONTRACT_FIRST, preferred_element_type=jnp.float32
    )
    d_gate = (d_hidden * up_act * gate_sigmoid * (1.0 + gate_act * (1.0 - gate_sigmoid))).astype(
        jnp.bfloat16
    )
    d_up = (d_hidden * gate_silu).astype(jnp.bfloat16)
    grad_gate = lax.dot_general(xn_two, d_gate, CONTRACT_FIRST, preferred_element_type=jnp.float32)
    grad_up = lax.dot_general(xn_two, d_up, CONTRACT_FIRST, preferred_element_type=jnp.float32)
    dn_two_part = lax.dot_general(
        d_gate, w_gate, CONTRACT_LAST, preferred_element_type=jnp.float32
    ) + lax.dot_general(d_up, w_up, CONTRACT_LAST, preferred_element_type=jnp.float32)
    dn_two = lax.psum(dn_two_part, "mp")
    back_two, _ = norm_back(dn_two, hidden_full, gain_two)
    dh_full = out_grad.astype(jnp.float32) + back_two
    dh_rows = lax.dynamic_slice_in_dim(dh_full, row_first, shard_rows, 0)
    grad_gain_two = jnp.sum(
        lax.dynamic_slice_in_dim(dn_two, row_first, shard_rows, 0) * normalize(hidden_rows), axis=0
    )
    dh_low = dh_full.astype(jnp.bfloat16)
    grad_out_proj = lax.dot_general(
        attended, dh_low, CONTRACT_FIRST, preferred_element_type=jnp.float32
    )
    d_att = lax.dot_general(dh_low, w_out, CONTRACT_LAST, preferred_element_type=jnp.float32)
    d_att = d_att.astype(jnp.bfloat16).reshape(row_count, heads_dev, head_size)
    dq_blocks = []
    d_keys = jnp.zeros((row_count, heads_dev, head_size), jnp.float32)
    d_values = jnp.zeros((row_count, heads_dev, head_size), jnp.float32)
    for block_index, row_start in enumerate(range(0, row_count, block_rows)):
        key_stop = row_start + block_rows
        scores = block_scores(row_start, key_stop)
        attn_probs = jnp.exp(scores - block_lse[block_index])
        probs_low = attn_probs.astype(jnp.bfloat16)
        att_rows = d_att[row_start:key_stop]
        d_probs = jnp.einsum(
            "qhe,khe->hqk", att_rows, v_low[:key_stop], preferred_element_type=jnp.float32
        )
        d_scores = (
            attn_probs * (d_probs - jnp.sum(d_probs * attn_probs, axis=-1, keepdims=True))
        ).astype(jnp.bfloat16)
        dq_blocks.append(
            jnp.einsum(
                "hqk,khe->qhe", d_scores, k_rot[:key_stop], preferred_element_type=jnp.float32
            )
            * score_scale
        )
        d_keys = d_keys.at[:key_stop].add(
            jnp.einsum(
                "hqk,qhe->khe",
                d_scores,
                q_rot[row_start:key_stop],
                preferred_element_type=jnp.float32,
            )
            * score_scale
        )
        d_values = d_values.at[:key_stop].add(
            jnp.einsum("hqk,qhe->khe", probs_low, att_rows, preferred_element_type=jnp.float32)
        )
    d_queries = jnp.concatenate(dq_blocks, axis=0)
    dq_raw, grad_q_gain = norm_back(rotate(d_queries, cosine_tab, sine_tab, -1.0), q_raw, q_gain_f)
    dk_raw, grad_k_gain = norm_back(rotate(d_keys, cosine_tab, sine_tab, -1.0), k_raw, k_gain_f)
    d_proj = jnp.concatenate(
        [
            dq_raw.reshape(row_count, head_span),
            dk_raw.reshape(row_count, head_span),
            d_values.reshape(row_count, head_span),
        ],
        axis=1,
    ).astype(jnp.bfloat16)
    w_proj = jnp.concatenate([w_query, spread(key_cols), spread(value_cols)], axis=1)
    dn_one_part = lax.dot_general(d_proj, w_proj, CONTRACT_LAST, preferred_element_type=jnp.float32)
    grad_proj = lax.dot_general(xn_one, d_proj, CONTRACT_FIRST, preferred_element_type=jnp.float32)
    grad_query = grad_proj[:, :head_span]
    grad_keyval = jnp.zeros((model_width, 2 * kv_heads * head_size), jnp.float32)
    grad_keyval = lax.dynamic_update_slice_in_dim(
        grad_keyval, fold_heads(grad_proj[:, head_span : 2 * head_span]), kv_first * head_size, 1
    )
    grad_keyval = lax.dynamic_update_slice_in_dim(
        grad_keyval, fold_heads(grad_proj[:, 2 * head_span :]), (kv_heads + kv_first) * head_size, 1
    )
    dn_one_rows = lax.psum_scatter(
        dn_one_part.astype(jnp.bfloat16), "mp", scatter_dimension=0, tiled=True
    ).astype(jnp.float32)
    back_one, grad_gain_one = norm_back(dn_one_rows, x_rows, gain_one)
    grad_tokens = dh_rows + back_one
    grad_query, grad_out_proj, grad_gate, grad_up, grad_down = (
        lax.psum_scatter(
            grad_query.astype(jnp.bfloat16), "dp", scatter_dimension=0, tiled=True
        ).astype(jnp.float32),
        lax.psum_scatter(
            grad_out_proj.astype(jnp.bfloat16), "dp", scatter_dimension=1, tiled=True
        ).astype(jnp.float32),
        lax.psum_scatter(
            grad_gate.astype(jnp.bfloat16), "dp", scatter_dimension=0, tiled=True
        ).astype(jnp.float32),
        lax.psum_scatter(
            grad_up.astype(jnp.bfloat16), "dp", scatter_dimension=0, tiled=True
        ).astype(jnp.float32),
        lax.psum_scatter(
            grad_down.astype(jnp.bfloat16), "dp", scatter_dimension=1, tiled=True
        ).astype(jnp.float32),
    )
    grad_keyval = lax.psum_scatter(grad_keyval, ("dp", "mp"), scatter_dimension=0, tiled=True)
    grad_gain_one, grad_gain_two, grad_q_gain, grad_k_gain = lax.psum(
        (grad_gain_one, grad_gain_two, grad_q_gain, grad_k_gain), ("dp", "mp")
    )
    return (
        block_out,
        grad_tokens,
        grad_gain_one,
        grad_query,
        grad_keyval,
        grad_q_gain,
        grad_k_gain,
        grad_out_proj,
        grad_gain_two,
        grad_gate,
        grad_up,
        grad_down,
    )


def solution(mesh):
    return jax.shard_map(
        shards,
        mesh=mesh,
        in_specs=(
            P("dp", None),
            P("dp", None),
            P("mp"),
            P(),
            P(None, "mp"),
            P(),
            P(),
            P(),
            P("mp", None),
            P(),
            P(None, "mp"),
            P(None, "mp"),
            P("mp", None),
            P("dp", None),
        ),
        out_specs=(
            P(("dp", "mp"), None),
            P(("dp", "mp"), None),
            P(),
            P("dp", "mp"),
            P(("dp", "mp"), None),
            P(),
            P(),
            P("mp", "dp"),
            P(),
            P("dp", "mp"),
            P("dp", "mp"),
            P("mp", "dp"),
        ),
        check_vma=False,
    )
```

profile of v0, /device:TPU:0, one launch (start us, length us, event | category | flops | bytes accessed | tf_op | source)
XLA Modules:
  0.0 1244.2 jit_solution(17080760547115743847)
XLA Ops:
  8.2 3.3 multiply_reduce_fusion.3
  11.6 3.5 fusion.103
  15.3 4.5 constant_dynamic-slice_fusion.1
  19.9 2.6 copy.165
  22.5 2.2 copy.164
  24.7 4.5 fusion.45
  34.5 2.9 fusion.58
  41.0 2.4 fusion.108
  43.5 3.0 fusion
  48.0 3.6 fusion.68
  56.8 5.6 fusion.110
  63.2 292.8 %all-reduce.6.cloned.1.call-done = f32[1024,2048]{1,0:T(8,128)} async-done(((f32[1024,2048]{1,0:T(8,128)}), f32[1024,2048]{1,0:T(8,128)}) %all-reduce.6.cloned.1.call-update) | async-done | bytes 8388624 | tf_op jit(solution)/shard_map/psum | solution.py:173
  356.0 5.7 multiply_reduce_fusion.2
  362.5 2.4 copy-done.2
  364.9 11.4 fusion.111
  376.4 7.3 fusion.112
  383.7 12.7 %multiply_convert_fusion.4 = (bf16[1024,1152]{1,0:T(8,128)(2,1)S(1)}, bf16[1024,1152]{1,0:T(8,128)(2,1)}, bf16[1024,1152]{1,0:T(8,128)(2,1)}) fusion(f32[1024,1152]{1,0:T(8,128)} %fusion.111, f32[1024,1152]{1,0:T(8,128)} %fusion.112, f32[1152]{0:T(1024)S(1)} %broadcast_bitcast_fusion, bf16[1024,2048]{1,0:T(8,128)(2,1)S(1)} %copy-done.27, ...), kind=kOutput, calls=%fused_computation.36 | convolution fusion | flops 4851892224 | bytes 25432576 | tf_op jit(solution)/shard_map/dot_general | solution.py:188
  396.5 8.1 fusion.113
  404.6 8.5 convolution_add_fusion
  413.3 9.6 convolution_convert_fusion.2
  422.9 9.6 convolution_convert_fusion.1
  432.6 9.2 convolution_convert_fusion
  442.5 9.5 convolution_convert_fusion.3
  452.1 251.1 %all-reduce.8.cloned.1.call-done = f32[1024,2048]{1,0:T(8,128)} async-done(((f32[1024,2048]{1,0:T(8,128)}), f32[1024,2048]{1,0:T(8,128)}) %all-reduce.8.cloned.1.call-update) | async-done | bytes 8388624 | tf_op jit(solution)/shard_map/psum | solution.py:203
  703.2 6.9 multiply_reduce_fusion.1
  713.0 8.3 multiply_add_fusion
  721.3 5.3 fusion.55
  727.4 4.7 multiply_reduce_fusion.4
  732.1 4.8 multiply_convert_fusion.3
  737.0 2.7 fusion.64
  739.6 2.9 fusion.62
  742.6 6.3 multiply_reduce_fusion
  748.9 6.9 multiply_convert_fusion
  757.1 2.1 fusion.63
  766.0 2.8 fusion.49
  768.8 5.3 fusion.73
  774.2 3.7 copy-done.14
  779.3 6.4 convolution_convert_fusion.6
  785.8 2.7 copy.152
  792.5 7.4 fusion.19
  800.1 5.2 fusion.104
  805.3 3.7 fusion.26
  811.8 5.7 fusion.29
  818.4 1.8 copy.158
  820.2 3.0 broadcast_in_dim.37
  823.2 11.5 dynamic_update_slice.6
  834.7 11.0 dynamic_update_slice.7
  845.8 6.5 convert_element_type.145
  852.3 1.8 multiply_reduce_fusion.7
  854.1 1.8 multiply_reduce_fusion.6
  856.0 2.2 convert_element_type.185
  858.1 2.2 convert_element_type.187
  860.3 13.2 %reduce-scatter.23.cloned.1.call-done = bf16[1152,256]{1,0:T(8,128)(2,1)} async-done(((bf16[1152,2048]{1,0:T(8,128)(2,1)}), bf16[1152,256]{1,0:T(8,128)(2,1)}) %reduce-scatter.23.cloned.1.call-update) | async-done | bytes 589840 | tf_op jit(solution)/shard_map/reduce_scatter | solution.py:289
  873.6 2.2 convert_element_type.189
  875.8 76.7 %reduce-scatter.9.cloned.1.call-done = bf16[256,2048]{1,0:T(8,128)(2,1)} async-done(((bf16[1024,2048]{1,0:T(8,128)(2,1)}), bf16[256,2048]{1,0:T(8,128)(2,1)}) %reduce-scatter.9.cloned.1.call-update) | async-done | bytes 1048592 | tf_op jit(solution)/shard_map/reduce_scatter | solution.py:183
  952.5 4.0 multiply_reduce_fusion.5
  956.6 38.2 %reduce-scatter.13.cloned.1.call-done = bf16[256,384]{0,1:T(8,128)(2,1)} async-done(((bf16[2048,384]{0,1:T(8,128)(2,1)}), bf16[256,384]{0,1:T(8,128)(2,1)}) %reduce-scatter.13.cloned.1.call-update) | async-done | bytes 196624 | tf_op jit(solution)/shard_map/reduce_scatter | solution.py:277
  994.7 1.8 copy.159
  996.5 39.9 %reduce-scatter.17.cloned.1.call-done = bf16[384,256]{1,0:T(8,128)(2,1)} async-done(((bf16[384,2048]{1,0:T(8,128)(2,1)}), bf16[384,256]{1,0:T(8,128)(2,1)}) %reduce-scatter.17.cloned.1.call-update) | async-done | bytes 196624 | tf_op jit(solution)/shard_map/reduce_scatter | solution.py:280
  1038.1 77.4 %reduce-scatter.11.cloned.1.call-done = bf16[256,2048]{1,0:T(8,128)(2,1)} async-done(((bf16[1024,2048]{1,0:T(8,128)(2,1)}), bf16[256,2048]{1,0:T(8,128)(2,1)}) %reduce-scatter.11.cloned.1.call-update) | async-done | bytes 1048592 | tf_op jit(solution)/shard_map/reduce_scatter | solution.py:271
  1115.5 2.7 fusion.39
  1118.2 41.1 %all-reduce.2 = (f32[2048]{0:T(1024)}, f32[64]{0:T(128)}, f32[64]{0:T(128)}, f32[2048]{0:T(1024)}) all-reduce(f32[2048]{0:T(1024)S(1)} %get-tuple-element.124, f32[64]{0:T(128)S(1)} %reduce_sum.217, f32[64]{0:T(128)S(1)} %get-tuple-element.126, f32[2048]{0:T(1024)S(1)} %get-tuple-element.141), channel_id=1, replica_groups=mesh['dp'=8,'mp'=4] {'dp','mp'}, use_global_device_ids=true, to_apply=%region_23.24 | all-reduce | flops 4224 | bytes 33792 | tf_op jit(solution)/shard_map/psum | solution.py:294
  1159.3 4.6 fusion.38
  1163.9 73.2 %reduce-scatter.15.cloned.1.call-done = f32[64,768]{1,0:T(8,128)} async-done(((f32[2048,768]{1,0:T(8,128)}), f32[64,768]{1,0:T(8,128)}) %reduce-scatter.15.cloned.1.call-update) | async-done | bytes 196624 | tf_op jit(solution)/shard_map/reduce_scatter | solution.py:293
  (249 shorter events, 41.8 us)
Async XLA Ops:
  7.2 49.6 %copy-start = (bf16[384,2048]{1,0:T(8,128)(2,1)S(1)}, bf16[384,2048]{1,0:T(8,128)(2,1)}, u32[]{:S(2)}) copy-start(bf16[384,2048]{1,0:T(8,128)(2,1)} %param.34) | copy-start | bytes 4718596
  7.2 4.3 copy-start.64
  7.2 348.8 %all-reduce.6.cloned.1.call-start = ((), (), s32[]{:S(2)}) async-start(), calls=%async_computation.8 | async-start | bytes 16777216 | tf_op jit(solution)/shard_map/psum | solution.py:173
  7.3 4.3 copy-start.8
  7.3 27.2 %copy-start.54 = (s32[6]{0:T(128)}, s32[6]{0:T(128)S(1)}, u32[]{:S(2)}) copy-start(s32[6]{0:T(128)S(1)} %fusion.88) | copy-start | bytes 76
  8.2 16.5 %copy-start.52 = (f32[2048]{0:T(1024)}, f32[2048]{0:T(1024)S(1)}, u32[]{:S(2)}) copy-start(f32[2048]{0:T(1024)S(1)} %convert_element_type.146) | copy-start | bytes 24580
  11.5 13.2 %copy-start.59 = (f32[1024]{0:T(1024)}, f32[1024]{0:T(1024)S(1)}, u32[]{:S(2)}) copy-start(f32[1024]{0:T(1024)S(1)} %add_rsqrt_fusion.3) | copy-start | bytes 12292
  11.6 27.6 %copy-start.61 = (f32[64]{0:T(128)}, f32[64]{0:T(128)S(1)}, u32[]{:S(2)}) copy-start(f32[64]{0:T(128)S(1)} %convert_element_type.151) | copy-start | bytes 772
  11.6 3.7 copy-start.66
  15.1 24.2 %copy-start.10 = (f32[1024,384]{0,1:T(8,128)}, f32[1024,384]{0,1:T(8,128)S(1)}, u32[]{:S(2)}) copy-start(f32[1024,384]{0,1:T(8,128)S(1)} %fusion.103) | copy-start | bytes 4718596
  15.3 23.9 %copy-start.45 = (f32[1024,6]{0,1:T(8,128)}, f32[1024,6]{0,1:T(8,128)S(1)}, u32[]{:S(2)}) copy-start(f32[1024,6]{0,1:T(8,128)S(1)} %add_rsqrt_fusion.1) | copy-start | bytes 73732
  15.3 23.9 %copy-start.56 = (f32[64]{0:T(128)}, f32[64]{0:T(128)S(1)}, u32[]{:S(2)}) copy-start(f32[64]{0:T(128)S(1)} %convert_element_type.153) | copy-start | bytes 772
  29.2 4.9 copy-start.63
  34.1 6.3 copy-start.47
  34.3 4.9 copy-start.5
  37.4 9.1 copy-start.23
  37.4 16.6 %copy-start.36 = (bf16[512,6,64]{0,1,2:T(8,128)(2,1)}, bf16[512,6,64]{0,1,2:T(8,128)(2,1)S(1)}, u32[]{:S(2)}) copy-start(bf16[512,6,64]{0,1,2:T(8,128)(2,1)S(1)} %slice.197) | copy-start | bytes 1179652
  41.0 10.9 copy-start.15
  41.0 10.9 copy-start.17
  41.0 10.9 copy-start.19
  41.0 10.9 copy-start.21
  43.5 4.5 copy-start.1
  62.5 640.7 %all-reduce.8.cloned.1.call-start = ((), (), s32[]{:S(2)}) async-start(), calls=%async_computation.10 | async-start | bytes 16777216 | tf_op jit(solution)/shard_map/psum | solution.py:203
  361.7 3.2 copy-start.2
  361.7 14.6 %slice-start.7 = ((s8[4718592]{0:T(1024)(128)(4,1)}), s8[524288]{0:T(1024)(128)(4,1)S(1)}, s32[]{:S(2)}) async-start(s8[4718592]{0:T(1024)(128)(4,1)} %bitcast.161), calls=%async_computation.25 | async-start | bytes 1048576
  364.9 11.4 copy-start.29
  364.9 11.4 slice-start.8
  376.3 7.4 copy-start.27
  376.4 20.1 %slice-start.5 = ((s8[4718592]{0:T(1024)(128)(4,1)}), s8[4194304]{0:T(1024)(128)(4,1)S(1)}, s32[]{:S(2)}) async-start(s8[4718592]{0:T(1024)(128)(4,1)} %bitcast.159), calls=%async_computation.23 | async-start | bytes 8388608
  376.4 28.3 %slice-start.9 = ((s8[4718592]{0:T(1024)(128)(4,1)}), s8[4194304]{0:T(1024)(128)(4,1)S(1)}, s32[]{:S(2)}) async-start(s8[4718592]{0:T(1024)(128)(4,1)} %bitcast.163), calls=%async_computation.27 | async-start | bytes 8388608
  383.7 12.7 %slice-start.6 = ((s8[4718592]{0:T(1024)(128)(4,1)}), s8[524288]{0:T(1024)(128)(4,1)S(1)}, s32[]{:S(2)}) async-start(s8[4718592]{0:T(1024)(128)(4,1)} %bitcast.159), calls=%async_computation.24 | async-start | bytes 1048576
  383.7 20.9 %slice-start.10 = ((s8[4718592]{0:T(1024)(128)(4,1)}), s8[524288]{0:T(1024)(128)(4,1)S(1)}, s32[]{:S(2)}) async-start(s8[4718592]{0:T(1024)(128)(4,1)} %bitcast.163), calls=%async_computation.28 | async-start | bytes 1048576
  396.5 8.2 copy-start.68
  413.2 442.8 %reduce-scatter.19.cloned.1.call-start = ((), (), s32[]{:S(2)}) async-start(), calls=%async_computation.15 | async-start | bytes 5308416 | tf_op jit(solution)/shard_map/reduce_scatter | solution.py:283
  422.9 435.3 %reduce-scatter.21.cloned.1.call-start = ((), (), s32[]{:S(2)}) async-start(), calls=%async_computation.16 | async-start | bytes 5308416 | tf_op jit(solution)/shard_map/reduce_scatter | solution.py:286
  432.5 441.0 %reduce-scatter.23.cloned.1.call-start = ((), (), s32[]{:S(2)}) async-start(), calls=%async_computation.17 | async-start | bytes 5308416 | tf_op jit(solution)/shard_map/reduce_scatter | solution.py:289
  441.8 510.8 %reduce-scatter.9.cloned.1.call-start = ((), (), s32[]{:S(2)}) async-start(), calls=%async_computation.9 | async-start | bytes 5242880 | tf_op jit(solution)/shard_map/reduce_scatter | solution.py:183
  442.5 284.9 %copy-start.50 = (f32[6,512]{1,0:T(8,128)}, f32[6,512]{1,0:T(8,128)S(1)}, u32[]{:S(2)}) copy-start(f32[6,512]{1,0:T(8,128)S(1)} %log_add_fusion.1) | copy-start | bytes 36868
  452.0 542.7 %reduce-scatter.13.cloned.1.call-start = ((), (), s32[]{:S(2)}) async-start(), calls=%async_computation.12 | async-start | bytes 1769472 | tf_op jit(solution)/shard_map/reduce_scatter | solution.py:277
  703.2 8.5 copy-start.7
  703.2 9.9 copy-start.28
  710.1 17.3 %slice-start.3 = ((s8[6291456]{0:T(1024)(128)(4,1)}), s8[4194304]{0:T(1024)(128)(4,1)S(1)}, s32[]{:S(2)}) async-start(s8[6291456]{0:T(1024)(128)(4,1)} %bitcast.132), calls=%async_computation.21 | async-start | bytes 8388608
  713.0 14.3 %slice-start.4 = ((s8[6291456]{0:T(1024)(128)(4,1)}), s8[2097152]{0:T(1024)(128)(4,1)S(1)}, s32[]{:S(2)}) async-start(s8[6291456]{0:T(1024)(128)(4,1)} %bitcast.132), calls=%async_computation.22 | async-start | bytes 4194304
  721.3 6.1 copy-start.37
  727.4 4.8 copy-start.30
  732.1 10.4 slice-start
  732.1 10.4 slice-start.1
  736.9 5.6 slice-start.2
  736.9 5.6 copy-start.24
  736.9 5.6 copy-start.32
  748.9 6.9 copy-start.18
  748.9 6.9 copy-start.35
  761.8 7.0 copy-start.43
  761.8 3.0 copy-start.31
  761.8 3.0 copy-start.51
  765.9 2.9 copy-start.9
  765.9 2.9 copy-start.53
  765.9 2.9 copy-start.60
  768.8 5.4 copy-start.41
  774.2 3.7 copy-start.14
  779.3 257.2 %reduce-scatter.17.cloned.1.call-start = ((), (), s32[]{:S(2)}) async-start(), calls=%async_computation.14 | async-start | bytes 1769472 | tf_op jit(solution)/shard_map/reduce_scatter | solution.py:280
  785.7 2.8 copy-start.55
  785.7 329.8 %reduce-scatter.11.cloned.1.call-start = ((), (), s32[]{:S(2)}) async-start(), calls=%async_computation.11 | async-start | bytes 5242880 | tf_op jit(solution)/shard_map/reduce_scatter | solution.py:271
  799.9 437.2 %reduce-scatter.15.cloned.1.call-start = ((), (), s32[]{:S(2)}) async-start(), calls=%async_computation.13 | async-start | bytes 6488064 | tf_op jit(solution)/shard_map/reduce_scatter | solution.py:293
  (26 other events, 43.4 us)
Sparse Core Ops, SparseCore 0:
  62.6 293.3 all-reduce.5
  413.3 289.8 all-reduce.7
  706.6 52.7 reduce-scatter.18
  762.7 53.7 reduce-scatter.20
  819.9 53.6 reduce-scatter.22
  875.7 76.7 reduce-scatter.8
  955.8 38.8 reduce-scatter.12
  998.0 38.3 reduce-scatter.16
  1038.7 76.7 reduce-scatter.10
  1121.6 115.4 reduce-scatter.14
where the time goes:
time: 1250 us; the launch traced here: 1240 us
  waiting for transfers between devices  863 us (69%)
  matrix products  172 us (14%)
  other arithmetic  80.4 us (6%)
  local copies, waits for them, and re-layouts  71.4 us (6%)
  blocking collectives  41.1 us (3%)
  between operations  15.7 us (1%)
    psum x1, waiting for transfers between devices, shards(): hidden_full = x_float + lax.psum(attn_part, 'mp')  293 us
    psum x1, waiting for transfers between devices, shards(): dn_two = lax.psum(dn_two_part, 'mp')  251 us
    reduce_scatter x1, waiting for transfers between devices, shards(): lax.psum_scatter(dn_one_part.astype(jnp.bfloat16), 'mp', scatter_dimensio...  77.4 us
    reduce_scatter x1, waiting for transfers between devices, shards(): lax.psum_scatter(ffn_part.astype(jnp.bfloat16), 'mp', scatter_dimension=0...  76.7 us
    reduce_scatter x1, waiting for transfers between devices, shards(): lax.psum_scatter(grad_keyval, ('dp', 'mp'), scatter_dimension=0, tiled=True)  73.2 us
    psum x1, blocking collectives, shards(): lax.psum((grad_gain_one, grad_gain_two, grad_q_gain, grad_k_gain), ('dp',...  41.1 us
    reduce_scatter x1, waiting for transfers between devices, shards(): lax.psum_scatter(grad_out_proj.astype(jnp.bfloat16), 'dp', scatter_dimens...  39.9 us
    reduce_scatter x1, waiting for transfers between devices, shards(): lax.psum_scatter(grad_query.astype(jnp.bfloat16), 'dp', scatter_dimension...  38.2 us
  transfers between devices with their start and end apart: 10, of which 8 were waited for; matrix products, arithmetic and copies ran while one was open for 16% of the time, Pallas kernels for 0%

commit v1 on v0

--- a/solution.py
+++ b/solution.py
@@ -170,7 +170,7 @@
         jnp.concatenate(block_outs, axis=0).reshape(row_count, head_span).astype(jnp.bfloat16)
     )
     attn_part = jnp.dot(attended, w_out, preferred_element_type=jnp.float32)
-    hidden_full = x_float + lax.psum(attn_part, "mp")
+    hidden_full = x_float + jnp.sum(jax.lax.all_gather(attn_part, "mp"), axis=0)
     hidden_rows = lax.dynamic_slice_in_dim(hidden_full, row_first, shard_rows, 0)
     xn_two = (normalize(hidden_full) * gain_two).astype(jnp.bfloat16)
     live_cols = jnp.repeat(slot_live.astype(jnp.float32), tile_cols)

time: 1250 us -> 1530 us (1.22)
  waiting for transfers between devices: 863 us -> 1130 us
  other arithmetic: 80.4 us -> 96.9 us
    all_gather x0 -> x1, waiting for transfers between devices: none -> 563 us  [shards(): hidden_full = x_float + jnp.sum(jax.lax.all_gather(attn_part, 'mp'), axis=0)]
    psum x1 -> x0, waiting for transfers between devices: 293 us -> none  [shards(): hidden_full = x_float + lax.psum(attn_part, 'mp')]
    reduce_sum x0 -> x1, other arithmetic: none -> 16.4 us  [shards(): hidden_full = x_float + jnp.sum(jax.lax.all_gather(attn_part, 'mp'), axis=0)]
  transfers between devices with their start and end apart: 10 -> 10, of which waited for: 8 -> 8; matrix products, arithmetic and copies ran while one was open for 16% -> 13% of each run, Pallas kernels for 0% -> 0%
where the time goes in v1:
time: 1530 us
  waiting for transfers between devices  1130 us (74%)
  matrix products  171 us (11%)
  other arithmetic  96.9 us (6%)
  local copies, waits for them, and re-layouts  71.2 us (5%)
  blocking collectives  41.1 us (3%)
  between operations  15.7 us (1%)
    all_gather x1, waiting for transfers between devices, shards(): hidden_full = x_float + jnp.sum(jax.lax.all_gather(attn_part, 'mp'), axis=0)  563 us
    psum x1, waiting for transfers between devices, shards(): dn_two = lax.psum(dn_two_part, 'mp')  250 us
    reduce_scatter x1, waiting for transfers between devices, shards(): lax.psum_scatter(dn_one_part.astype(jnp.bfloat16), 'mp', scatter_dimensio...  77.4 us
    reduce_scatter x1, waiting for transfers between devices, shards(): lax.psum_scatter(ffn_part.astype(jnp.bfloat16), 'mp', scatter_dimension=0...  76.7 us
    reduce_scatter x1, waiting for transfers between devices, shards(): lax.psum_scatter(grad_keyval, ('dp', 'mp'), scatter_dimension=0, tiled=True)  73.2 us
    psum x1, blocking collectives, shards(): lax.psum((grad_gain_one, grad_gain_two, grad_q_gain, grad_k_gain), ('dp',...  41.1 us
    reduce_scatter x1, waiting for transfers between devices, shards(): lax.psum_scatter(grad_out_proj.astype(jnp.bfloat16), 'dp', scatter_dimens...  39.9 us
    reduce_scatter x1, waiting for transfers between devices, shards(): lax.psum_scatter(grad_query.astype(jnp.bfloat16), 'dp', scatter_dimension...  38.1 us
  transfers between devices with their start and end apart: 10, of which 8 were waited for; matrix products, arithmetic and copies ran while one was open for 13% of the time, Pallas kernels for 0%

profile of v1, /device:TPU:0, one launch (start us, length us, event | category | flops | bytes accessed | tf_op | source)
XLA Modules:
  0.0 1529.2 jit_solution(7573559613667876894)
XLA Ops:
  8.2 3.3 multiply_reduce_fusion.3
  11.6 3.5 fusion.103
  15.3 4.5 constant_dynamic-slice_fusion.1
  19.9 2.3 copy.165
  22.2 2.2 copy.164
  24.4 4.5 fusion.45
  34.2 2.9 fusion.58
  40.7 2.4 fusion.108
  43.2 3.0 fusion
  47.7 3.6 fusion.68
  56.5 5.7 fusion.110
  62.9 563.3 %all-gather.3.cloned.1.call-done = f32[4096,2048]{1,0:T(8,128)} async-done(((f32[1024,2048]{1,0:T(8,128)}), f32[4096,2048]{1,0:T(8,128)}) %all-gather.3.cloned.1.call-update) | async-done | bytes 33554448 | tf_op jit(solution)/shard_map/all_gather | solution.py:173
  626.3 16.4 %reduce_sum.215 = f32[1024,2048]{1,0:T(8,128)} reduce(f32[4,1024,2048]{2,1,0:T(8,128)} %bitcast.135, f32[]{:T(128)} %constant.179.clone.1), dimensions={0}, to_apply=%region_10.11 | reduce | flops 6291456 | bytes 41943044 | tf_op jit(solution)/shard_map/reduce_sum | solution.py:173
  642.7 5.7 multiply_reduce_fusion.2
  649.2 2.4 copy-done.2
  651.6 11.0 fusion.111
  662.7 7.3 fusion.112
  670.0 12.8 multiply_convert_fusion.4
  682.9 8.1 fusion.113
  691.1 8.0 convolution_add_fusion
  699.1 9.6 convolution_convert_fusion.2
  708.8 9.6 convolution_convert_fusion.1
  718.5 9.3 convolution_convert_fusion
  728.5 9.5 convolution_convert_fusion.3
  738.1 250.1 %all-reduce.5.cloned.1.call-done = f32[1024,2048]{1,0:T(8,128)} async-done(((f32[1024,2048]{1,0:T(8,128)}), f32[1024,2048]{1,0:T(8,128)}) %all-reduce.5.cloned.1.call-update) | async-done | bytes 8388624 | tf_op jit(solution)/shard_map/psum | solution.py:203
  988.3 6.7 multiply_reduce_fusion.1
  998.1 8.3 multiply_add_fusion
  1006.4 5.3 fusion.55
  1012.5 4.8 multiply_reduce_fusion.4
  1017.3 4.8 multiply_convert_fusion.3
  1022.1 2.7 fusion.64
  1024.7 2.9 fusion.62
  1027.7 6.3 multiply_reduce_fusion
  1034.0 7.1 multiply_convert_fusion
  1042.4 2.1 fusion.63
  1051.3 2.5 fusion.49
  1053.8 5.3 fusion.73
  1059.2 3.7 copy-done.14
  1064.3 6.3 convolution_convert_fusion.6
  1070.7 2.8 copy.152
  1077.5 7.4 fusion.19
  1085.2 5.2 fusion.104
  1090.5 3.7 fusion.26
  1096.9 5.7 fusion.29
  1103.5 1.8 copy.158
  1105.3 3.0 broadcast_in_dim.37
  1108.3 11.5 dynamic_update_slice.6
  1119.8 11.0 dynamic_update_slice.7
  1130.9 6.5 convert_element_type.145
  1137.4 1.8 multiply_reduce_fusion.7
  1139.2 1.8 multiply_reduce_fusion.6
  1141.1 2.2 convert_element_type.185
  1143.2 2.2 convert_element_type.187
  1145.4 13.2 reduce-scatter.23.cloned.1.call-done
  1158.6 2.2 convert_element_type.189
  1160.9 76.7 %reduce-scatter.9.cloned.1.call-done = bf16[256,2048]{1,0:T(8,128)(2,1)} async-done(((bf16[1024,2048]{1,0:T(8,128)(2,1)}), bf16[256,2048]{1,0:T(8,128)(2,1)}) %reduce-scatter.9.cloned.1.call-update) | async-done | bytes 1048592 | tf_op jit(solution)/shard_map/reduce_scatter | solution.py:183
  1237.6 4.0 multiply_reduce_fusion.5
  1241.6 38.1 %reduce-scatter.13.cloned.1.call-done = bf16[256,384]{0,1:T(8,128)(2,1)} async-done(((bf16[2048,384]{0,1:T(8,128)(2,1)}), bf16[256,384]{0,1:T(8,128)(2,1)}) %reduce-scatter.13.cloned.1.call-update) | async-done | bytes 196624 | tf_op jit(solution)/shard_map/reduce_scatter | solution.py:277
  1281.6 39.9 %reduce-scatter.17.cloned.1.call-done = bf16[384,256]{1,0:T(8,128)(2,1)} async-done(((bf16[384,2048]{1,0:T(8,128)(2,1)}), bf16[384,256]{1,0:T(8,128)(2,1)}) %reduce-scatter.17.cloned.1.call-update) | async-done | bytes 196624 | tf_op jit(solution)/shard_map/reduce_scatter | solution.py:280
  1323.1 77.4 %reduce-scatter.11.cloned.1.call-done = bf16[256,2048]{1,0:T(8,128)(2,1)} async-done(((bf16[1024,2048]{1,0:T(8,128)(2,1)}), bf16[256,2048]{1,0:T(8,128)(2,1)}) %reduce-scatter.11.cloned.1.call-update) | async-done | bytes 1048592 | tf_op jit(solution)/shard_map/reduce_scatter | solution.py:271
  1400.5 2.7 fusion.39
  1403.2 41.1 %all-reduce.2 = (f32[2048]{0:T(1024)}, f32[64]{0:T(128)}, f32[64]{0:T(128)}, f32[2048]{0:T(1024)}) all-reduce(f32[2048]{0:T(1024)S(1)} %get-tuple-element.124, f32[64]{0:T(128)S(1)} %reduce_sum.227, f32[64]{0:T(128)S(1)} %get-tuple-element.126, f32[2048]{0:T(1024)S(1)} %get-tuple-element.141), channel_id=1, replica_groups=mesh['dp'=8,'mp'=4] {'dp','mp'}, use_global_device_ids=true, to_apply=%region_23.24 | all-reduce | flops 4224 | bytes 33792 | tf_op jit(solution)/shard_map/psum | solution.py:294
  1444.3 4.6 fusion.38
  1448.9 73.2 %reduce-scatter.15.cloned.1.call-done = f32[64,768]{1,0:T(8,128)} async-done(((f32[2048,768]{1,0:T(8,128)}), f32[64,768]{1,0:T(8,128)}) %reduce-scatter.15.cloned.1.call-update) | async-done | bytes 196624 | tf_op jit(solution)/shard_map/reduce_scatter | solution.py:293
  (250 shorter events, 43.8 us)
Async XLA Ops:
  7.2 49.3 %copy-start = (bf16[384,2048]{1,0:T(8,128)(2,1)S(1)}, bf16[384,2048]{1,0:T(8,128)(2,1)}, u32[]{:S(2)}) copy-start(bf16[384,2048]{1,0:T(8,128)(2,1)} %param.34) | copy-start | bytes 4718596
  7.2 4.3 copy-start.64
  7.2 619.0 %all-gather.3.cloned.1.call-start = ((), (), s32[]{:S(2)}) async-start(), calls=%async_computation.17 | async-start | bytes 41943040 | tf_op jit(solution)/shard_map/all_gather | solution.py:173
  7.3 4.3 copy-start.8
  7.3 26.9 %copy-start.54 = (s32[6]{0:T(128)}, s32[6]{0:T(128)S(1)}, u32[]{:S(2)}) copy-start(s32[6]{0:T(128)S(1)} %fusion.88) | copy-start | bytes 76
  8.2 16.2 %copy-start.52 = (f32[2048]{0:T(1024)}, f32[2048]{0:T(1024)S(1)}, u32[]{:S(2)}) copy-start(f32[2048]{0:T(1024)S(1)} %convert_element_type.146) | copy-start | bytes 24580
  11.5 12.9 copy-start.59
  11.6 27.4 %copy-start.61 = (f32[64]{0:T(128)}, f32[64]{0:T(128)S(1)}, u32[]{:S(2)}) copy-start(f32[64]{0:T(128)S(1)} %convert_element_type.151) | copy-start | bytes 772
  11.6 3.7 copy-start.66
  15.1 23.9 %copy-start.10 = (f32[1024,384]{0,1:T(8,128)}, f32[1024,384]{0,1:T(8,128)S(1)}, u32[]{:S(2)}) copy-start(f32[1024,384]{0,1:T(8,128)S(1)} %fusion.103) | copy-start | bytes 4718596
  15.3 23.6 %copy-start.45 = (f32[1024,6]{0,1:T(8,128)}, f32[1024,6]{0,1:T(8,128)S(1)}, u32[]{:S(2)}) copy-start(f32[1024,6]{0,1:T(8,128)S(1)} %add_rsqrt_fusion.1) | copy-start | bytes 73732
  15.3 23.6 %copy-start.56 = (f32[64]{0:T(128)}, f32[64]{0:T(128)S(1)}, u32[]{:S(2)}) copy-start(f32[64]{0:T(128)S(1)} %convert_element_type.153) | copy-start | bytes 772
  29.0 4.9 copy-start.63
  33.8 6.3 copy-start.47
  34.0 4.9 copy-start.5
  37.1 9.2 copy-start.23
  37.1 16.6 %copy-start.36 = (bf16[512,6,64]{0,1,2:T(8,128)(2,1)}, bf16[512,6,64]{0,1,2:T(8,128)(2,1)S(1)}, u32[]{:S(2)}) copy-start(bf16[512,6,64]{0,1,2:T(8,128)(2,1)S(1)} %slice.197) | copy-start | bytes 1179652
  40.7 10.9 copy-start.15
  40.7 10.9 copy-start.17
  40.7 10.9 copy-start.19
  40.7 10.9 copy-start.21
  43.2 4.5 copy-start.1
  52.8 2.6 copy-start.3
  62.2 926.1 %all-reduce.5.cloned.1.call-start = ((), (), s32[]{:S(2)}) async-start(), calls=%async_computation.9 | async-start | bytes 16777216 | tf_op jit(solution)/shard_map/psum | solution.py:203
  648.4 3.2 copy-start.2
  648.4 14.2 slice-start.7
  651.6 11.0 copy-start.29
  651.6 11.0 slice-start.8
  662.7 7.3 copy-start.27
  662.7 20.2 %slice-start.5 = ((s8[4718592]{0:T(1024)(128)(4,1)}), s8[4194304]{0:T(1024)(128)(4,1)S(1)}, s32[]{:S(2)}) async-start(s8[4718592]{0:T(1024)(128)(4,1)} %bitcast.161), calls=%async_computation.23 | async-start | bytes 8388608
  662.7 28.3 %slice-start.9 = ((s8[4718592]{0:T(1024)(128)(4,1)}), s8[4194304]{0:T(1024)(128)(4,1)S(1)}, s32[]{:S(2)}) async-start(s8[4718592]{0:T(1024)(128)(4,1)} %bitcast.165), calls=%async_computation.27 | async-start | bytes 8388608
  670.0 12.9 slice-start.6
  670.0 21.0 %slice-start.10 = ((s8[4718592]{0:T(1024)(128)(4,1)}), s8[524288]{0:T(1024)(128)(4,1)S(1)}, s32[]{:S(2)}) async-start(s8[4718592]{0:T(1024)(128)(4,1)} %bitcast.165), calls=%async_computation.28 | async-start | bytes 1048576
  682.9 8.2 copy-start.68
  699.1 442.0 %reduce-scatter.19.cloned.1.call-start = ((), (), s32[]{:S(2)}) async-start(), calls=%async_computation.14 | async-start | bytes 5308416 | tf_op jit(solution)/shard_map/reduce_scatter | solution.py:283
  708.8 434.5 %reduce-scatter.21.cloned.1.call-start = ((), (), s32[]{:S(2)}) async-start(), calls=%async_computation.15 | async-start | bytes 5308416 | tf_op jit(solution)/shard_map/reduce_scatter | solution.py:286
  718.4 440.2 %reduce-scatter.23.cloned.1.call-start = ((), (), s32[]{:S(2)}) async-start(), calls=%async_computation.16 | async-start | bytes 5308416 | tf_op jit(solution)/shard_map/reduce_scatter | solution.py:289
  727.8 509.8 %reduce-scatter.9.cloned.1.call-start = ((), (), s32[]{:S(2)}) async-start(), calls=%async_computation.8 | async-start | bytes 5242880 | tf_op jit(solution)/shard_map/reduce_scatter | solution.py:183
  728.5 284.0 %copy-start.50 = (f32[6,512]{1,0:T(8,128)}, f32[6,512]{1,0:T(8,128)S(1)}, u32[]{:S(2)}) copy-start(f32[6,512]{1,0:T(8,128)S(1)} %log_add_fusion.1) | copy-start | bytes 36868
  738.1 541.7 %reduce-scatter.13.cloned.1.call-start = ((), (), s32[]{:S(2)}) async-start(), calls=%async_computation.11 | async-start | bytes 1769472 | tf_op jit(solution)/shard_map/reduce_scatter | solution.py:277
  988.3 8.5 copy-start.7
  988.3 9.9 copy-start.28
  995.0 17.4 %slice-start.3 = ((s8[6291456]{0:T(1024)(128)(4,1)}), s8[4194304]{0:T(1024)(128)(4,1)S(1)}, s32[]{:S(2)}) async-start(s8[6291456]{0:T(1024)(128)(4,1)} %bitcast.133), calls=%async_computation.21 | async-start | bytes 8388608
  998.1 14.3 slice-start.4
  1006.4 6.1 copy-start.37
  1012.5 4.8 copy-start.30
  1017.2 10.4 slice-start
  1017.3 10.4 slice-start.1
  1022.0 2.7 copy-start.16
  1022.0 5.6 slice-start.2
  1022.0 5.6 copy-start.24
  1022.1 5.6 copy-start.32
  1034.0 7.1 copy-start.18
  1034.0 7.1 copy-start.35
  1047.1 6.7 copy-start.43
  1047.1 3.0 copy-start.31
  1047.1 3.0 copy-start.51
  1053.8 5.4 copy-start.41
  1059.2 3.7 copy-start.14
  1064.3 257.1 %reduce-scatter.17.cloned.1.call-start = ((), (), s32[]{:S(2)}) async-start(), calls=%async_computation.13 | async-start | bytes 1769472 | tf_op jit(solution)/shard_map/reduce_scatter | solution.py:280
  1070.7 2.8 copy-start.26
  1070.7 2.8 copy-start.55
  1070.7 329.9 %reduce-scatter.11.cloned.1.call-start = ((), (), s32[]{:S(2)}) async-start(), calls=%async_computation.10 | async-start | bytes 5242880 | tf_op jit(solution)/shard_map/reduce_scatter | solution.py:271
  1085.0 437.1 %reduce-scatter.15.cloned.1.call-start = ((), (), s32[]{:S(2)}) async-start(), calls=%async_computation.12 | async-start | bytes 6488064 | tf_op jit(solution)/shard_map/reduce_scatter | solution.py:293
  (26 other events, 43.0 us)
Sparse Core Ops, SparseCore 0:
  62.3 563.9 all-gather.2
  699.2 289.0 all-reduce.4
  991.7 52.7 reduce-scatter.18
  1047.8 53.7 reduce-scatter.20
  1104.9 53.6 reduce-scatter.22
  1160.8 76.7 reduce-scatter.8
  1240.9 38.8 reduce-scatter.12
  1283.0 38.3 reduce-scatter.16
  1323.7 76.7 reduce-scatter.10
  1406.6 115.4 reduce-scatter.14
